TPU v7x, 128 devices: a whole 4x4x4 slice. The times are simulated.
128 devices in a mesh: row: 8 (over x, core), col: 16 (over z, y).
Axes of the slice: x: 4, y: 4, z: 4, core: 2. Of those that a mesh axis runs over, the one named last changes fastest.
Arguments:
- matrix: float32 [8192, 8192], P('row', 'col'), as said below
- start_vectors: float32 [8192, 512], P(('col', 'row')), may hold values from -6 to 6
- interval: float32 [2], replicated, as said below
Outputs:
- ortho_basis: float32 [8192, 512], P(('col', 'row'))
- projected: float32 [512, 512], replicated
- residual: float32 [8192, 512], P(('col', 'row'))
Inputs may be any that keep to these rules, and one draw needn't show every extreme that they name: matrix is exactly symmetric (entry (r, c) equals entry (c, r)); its eigenvalues lie within about -1.45 to 1.45. interval[0] lies in [-1.2, -0.7] and interval[1] in [1.45, 1.9].
All inputs are finite; a program needn't handle non-finite values.
Results may differ from a plain program's by a relative error of at most 0.0003.
Values sent between devices are 32-bit elements.
A program may use at most 128 MiB of HBM per device.

v0:
```python
import jax
import jax.numpy as jnp
from jax import lax
from jax.sharding import Mesh
from jax.sharding import PartitionSpec as P

FILTER_DEG = 3
OUTER = 2
ROW = ("row_0", "row_1")
COL = ("col_0", "col_1")
ROW_COL = ("row_0", "row_1", "col_0", "col_1")
COL_ROW = ("col_0", "col_1", "row_0", "row_1")


def summed_rows(contribution, width, axes):
    total = contribution(jnp.int32(0), width * lax.axis_size(axes))
    for axis in axes:
        total = lax.psum_scatter(total, axis, scatter_dimension=0, tiled=True)
    return total


def whole_of(array, axes, dim):
    for axis in reversed(axes):
        array = lax.all_gather(array, axis, axis=dim, tiled=True)
    return array


def broadcast(array, axis, root):
    return lax.dynamic_index_in_dim(lax.all_gather(array, axis), root, 0, keepdims=False)


def over_pieces(array, axis):
    pieces = lax.all_gather(array, axis)
    return pieces.sum(axis=0)


def edges_of(length, count):
    unit = 8 if length >= 8 * count else 1
    return [length // unit * k // count * unit for k in range(1, count)]


def stacked_from(array, axes, turns):
    pieces = array
    for k in turns:
        pieces = lax.all_gather(pieces, axes[k])
    done = turns[::-1]
    back = [done.index(k) for k in range(len(axes))]
    pieces = pieces.transpose(*back, *range(len(axes), pieces.ndim))
    return pieces.reshape(-1, *array.shape)


def laid_out(pieces, dim):
    pieces = jnp.moveaxis(pieces, 0, dim)
    shape = pieces.shape
    return pieces.reshape(*shape[:dim], shape[dim] * shape[dim + 1], *shape[dim + 2 :])


def gather_all_axes(array, axes, dim):
    numbers = list(range(len(axes)))[::-1]
    widest = array.shape.index(max(array.shape[:-1] or array.shape))
    edges = [0, *edges_of(array.shape[widest], len(axes)), array.shape[widest]]
    finished = []
    for k, (start, end) in enumerate(zip(edges, edges[1:])):
        if end > start:
            share = lax.slice_in_dim(array, start, end, axis=widest)
            finished.append(stacked_from(share, axes, numbers[k:] + numbers[:k]))
    return laid_out(jnp.concatenate(finished, axis=widest + 1), dim)


def product(left, right):
    return jnp.dot(left, right, precision=lax.Precision.HIGHEST, preferred_element_type=jnp.float32)


def tri_solve(factor, values):
    return jax.scipy.linalg.solve_triangular(factor, values, lower=True)


def shards(matrix, start_vectors, interval):
    block_rows, block_cols = matrix.shape
    slab_rows = start_vectors.shape[0]
    total_rows = slab_rows * lax.axis_size(ROW) * lax.axis_size(COL)
    row_index = lax.axis_index(ROW)
    col_index = lax.axis_index(COL)
    center = 0.5 * (interval[0] + interval[1])
    half_width = 0.5 * (interval[1] - interval[0])
    global_rows = row_index * block_rows + lax.iota(jnp.int32, block_rows)
    global_cols = col_index * block_cols + lax.iota(jnp.int32, block_cols)
    diagonal = global_rows[:, None] == global_cols[None, :]
    shifted = jnp.where(diagonal, matrix - center, matrix) / half_width

    def forward(col_full):

        def term(first_row, row_count):
            strip = lax.dynamic_slice_in_dim(shifted, first_row, row_count, 0)
            return product(strip, col_full)

        return summed_rows(term, slab_rows, COL)

    def gather_rows(slab_part):
        return whole_of(slab_part, COL, 0)

    def to_columns(row_full):
        root_row = col_index * block_cols // block_rows
        offset = col_index * block_cols - root_row * block_rows
        column_part = lax.dynamic_slice_in_dim(row_full, offset, block_cols, 0)
        return broadcast(column_part, ROW, root_row)

    def backward(row_full):
        partial_value = lax.dot_general(
            shifted,
            row_full,
            (((0,), (0,)), ((), ())),
            precision=lax.Precision.HIGHEST,
            preferred_element_type=jnp.float32,
        )
        return over_pieces(partial_value, ROW)

    current_start = gather_all_axes(start_vectors, ROW, 0)
    for sweep_index in range(OUTER):
        even_cols = current_start
        odd_slab = forward(current_start)
        odd_rows = gather_rows(odd_slab)
        for degree in range(2, FILTER_DEG + 1):
            if degree % 2 == 0:
                even_cols = 2.0 * backward(odd_rows) - even_cols
            else:
                odd_slab = 2.0 * forward(even_cols) - odd_slab
                odd_rows = gather_rows(odd_slab)
        final_cols = to_columns(odd_rows)
        mapped_cols = backward(odd_rows)
        final_slab = lax.dynamic_slice_in_dim(final_cols, row_index * slab_rows, slab_rows, 0)
        mapped_slab = lax.dynamic_slice_in_dim(mapped_cols, row_index * slab_rows, slab_rows, 0)
        gram_part = product(final_slab.T, final_slab)
        cross_part = product(final_slab.T, mapped_slab)
        gram_total = lax.psum(gram_part, ROW_COL)
        cross_total = lax.psum(cross_part, ROW_COL)
        gram_matrix = gram_total / total_rows
        cross_terms = cross_total / total_rows
        factor = jnp.linalg.cholesky(gram_matrix)
        basis_cols = tri_solve(factor, final_cols.T).T
        partial_proj = tri_solve(factor, cross_terms)
        projected = tri_solve(factor, partial_proj.T).T
        current_start = basis_cols
    basis_slab = lax.dynamic_slice_in_dim(current_start, row_index * slab_rows, slab_rows, 0)
    residual = tri_solve(factor, mapped_slab.T).T - product(basis_slab, projected)
    return (basis_slab, projected, residual)


def solution(mesh):
    torus = Mesh(mesh.devices.reshape(4, 2, 4, 4), ("row_0", "row_1", "col_0", "col_1"))
    placed = (P(ROW, COL), P(COL_ROW, None), P())
    return jax.shard_map(
        shards,
        mesh=torus,
        in_specs=placed,
        out_specs=(P(COL_ROW, None), P(), P(COL_ROW, None)),
        check_vma=False,
    )
```

profile of v0, /device:TPU:1, one launch (start us, length us, event | category | flops | bytes accessed | tf_op | source)
XLA Modules:
  0.0 1350.0 jit_solution(3314252056546738000)
XLA Ops:
  46.1 33.9 %reduce-scatter.9.cloned.1.call-done = f32[256,512]{1,0:T(8,128)} async-done(((f32[1024,512]{1,0:T(8,128)}), f32[256,512]{1,0:T(8,128)}) %reduce-scatter.9.cloned.1.call-update) | async-done | bytes 524304 | tf_op jit(solution)/shard_map/reduce_scatter | solution.py:18
  80.0 21.3 %reduce-scatter.11.cloned.1.call-done = f32[64,512]{1,0:T(8,128)} async-done(((f32[256,512]{1,0:T(8,128)}), f32[64,512]{1,0:T(8,128)}) %reduce-scatter.11.cloned.1.call-update) | async-done | bytes 131088 | tf_op jit(solution)/shard_map/reduce_scatter | solution.py:18
  112.3 35.9 %all-gather.19.cloned.1.call-done = f32[1024,512]{1,0:T(8,128)} async-done(((f32[256,512]{1,0:T(8,128)}), f32[1024,512]{1,0:T(8,128)}) %all-gather.19.cloned.1.call-update) | async-done | bytes 2097168 | tf_op jit(solution)/shard_map/all_gather | solution.py:24
  155.3 49.6 %all-gather.27.cloned.1.call-done = f32[4096,512]{1,0:T(8,128)} async-done(((f32[512,512]{1,0:T(8,128)}), f32[4096,512]{1,0:T(8,128)}) %all-gather.27.cloned.1.call-update) | async-done | bytes 8388624 | tf_op jit(solution)/shard_map/all_gather | solution.py:33
  216.4 29.6 %reduce-scatter.13.cloned.1.call-done = f32[256,512]{1,0:T(8,128)} async-done(((f32[1024,512]{1,0:T(8,128)}), f32[256,512]{1,0:T(8,128)}) %reduce-scatter.13.cloned.1.call-update) | async-done | bytes 524304 | tf_op jit(solution)/shard_map/reduce_scatter | solution.py:18
  246.1 21.1 %reduce-scatter.15.cloned.1.call-done = f32[64,512]{1,0:T(8,128)} async-done(((f32[256,512]{1,0:T(8,128)}), f32[64,512]{1,0:T(8,128)}) %reduce-scatter.15.cloned.1.call-update) | async-done | bytes 131088 | tf_op jit(solution)/shard_map/reduce_scatter | solution.py:18
  268.1 12.0 all_gather.90
  280.2 34.5 %all-gather.21.cloned.1.call-done = f32[1024,512]{1,0:T(8,128)} async-done(((f32[256,512]{1,0:T(8,128)}), f32[1024,512]{1,0:T(8,128)}) %all-gather.21.cloned.1.call-update) | async-done | bytes 2097168 | tf_op jit(solution)/shard_map/all_gather | solution.py:24
  317.1 50.1 %all-gather.29.cloned.1.call-done = f32[4096,512]{1,0:T(8,128)} async-done(((f32[512,512]{1,0:T(8,128)}), f32[4096,512]{1,0:T(8,128)}) %all-gather.29.cloned.1.call-update) | async-done | bytes 8388624 | tf_op jit(solution)/shard_map/all_gather | solution.py:29
  373.3 148.4 %all-reduce.5.cloned.1.call-done = f32[512,512]{0,1:T(8,128)} async-done(((f32[512,512]{0,1:T(8,128)}), f32[512,512]{0,1:T(8,128)}) %all-reduce.5.cloned.1.call-update) | async-done | bytes 1048592 | tf_op jit(solution)/shard_map/psum | solution.py:135
  615.1 39.3 %custom-call.37 = f32[4,128,128]{1,2,0:T(8,128)S(1)} custom-call(f32[4,128,128]{2,1,0:T(8,128)S(1)} %get-tuple-element.39), custom_call_target="InvertDiagBlocksLowerTriangular" | custom-call | tf_op jit(solution)/shard_map/jit(_solve_triangular)/triangular_solve | solution.py:75
  662.8 28.1 %reduce-scatter.17.cloned.1.call-done = f32[256,512]{1,0:T(8,128)} async-done(((f32[1024,512]{1,0:T(8,128)}), f32[256,512]{1,0:T(8,128)}) %reduce-scatter.17.cloned.1.call-update) | async-done | bytes 524304 | tf_op jit(solution)/shard_map/reduce_scatter | solution.py:18
  690.9 21.3 %reduce-scatter.19.cloned.1.call-done = f32[64,512]{1,0:T(8,128)} async-done(((f32[256,512]{1,0:T(8,128)}), f32[64,512]{1,0:T(8,128)}) %reduce-scatter.19.cloned.1.call-update) | async-done | bytes 131088 | tf_op jit(solution)/shard_map/reduce_scatter | solution.py:18
  723.7 35.4 %all-gather.23.cloned.1.call-done = f32[1024,512]{1,0:T(8,128)} async-done(((f32[256,512]{1,0:T(8,128)}), f32[1024,512]{1,0:T(8,128)}) %all-gather.23.cloned.1.call-update) | async-done | bytes 2097168 | tf_op jit(solution)/shard_map/all_gather | solution.py:24
  766.3 50.1 %all-gather.31.cloned.1.call-done = f32[4096,512]{1,0:T(8,128)} async-done(((f32[512,512]{1,0:T(8,128)}), f32[4096,512]{1,0:T(8,128)}) %all-gather.31.cloned.1.call-update) | async-done | bytes 8388624 | tf_op jit(solution)/shard_map/all_gather | solution.py:33
  828.7 29.6 %reduce-scatter.21.cloned.1.call-done = f32[256,512]{1,0:T(8,128)} async-done(((f32[1024,512]{1,0:T(8,128)}), f32[256,512]{1,0:T(8,128)}) %reduce-scatter.21.cloned.1.call-update) | async-done | bytes 524304 | tf_op jit(solution)/shard_map/reduce_scatter | solution.py:18
  858.3 21.1 %reduce-scatter.23.cloned.1.call-done = f32[64,512]{1,0:T(8,128)} async-done(((f32[256,512]{1,0:T(8,128)}), f32[64,512]{1,0:T(8,128)}) %reduce-scatter.23.cloned.1.call-update) | async-done | bytes 131088 | tf_op jit(solution)/shard_map/reduce_scatter | solution.py:18
  880.3 12.0 all_gather.98
  892.4 34.5 %all-gather.25.cloned.1.call-done = f32[1024,512]{1,0:T(8,128)} async-done(((f32[256,512]{1,0:T(8,128)}), f32[1024,512]{1,0:T(8,128)}) %all-gather.25.cloned.1.call-update) | async-done | bytes 2097168 | tf_op jit(solution)/shard_map/all_gather | solution.py:24
  936.2 43.4 %all-gather.33.cloned.1.call-done = f32[4096,512]{1,0:T(8,128)} async-done(((f32[512,512]{1,0:T(8,128)}), f32[4096,512]{1,0:T(8,128)}) %all-gather.33.cloned.1.call-update) | async-done | bytes 8388624 | tf_op jit(solution)/shard_map/all_gather | solution.py:29
  982.6 48.3 %all-gather.35.cloned.1.call-done = f32[4096,512]{1,0:T(8,128)} async-done(((f32[512,512]{1,0:T(8,128)}), f32[4096,512]{1,0:T(8,128)}) %all-gather.35.cloned.1.call-update) | async-done | bytes 8388624 | tf_op jit(solution)/shard_map/all_gather | solution.py:33
  1041.0 150.0 %all-reduce.7.cloned.1.call-done = (f32[512,512]{0,1:T(8,128)}, f32[512,512]{0,1:T(8,128)}) async-done(((f32[512,512]{0,1:T(8,128)}, f32[512,512]{0,1:T(8,128)}), (f32[512,512]{0,1:T(8,128)}, f32[512,512]{0,1:T(8,128)})) %all-reduce.7.cloned.1.call-update) | async-done | bytes 2097168 | tf_op jit(solution)/shard_map/psum | solution.py:135
  1215.3 12.1 cholesky.377
  1285.0 39.5 %custom-call.41 = f32[4,128,128]{1,2,0:T(8,128)S(1)} custom-call(f32[4,128,128]{2,1,0:T(8,128)S(1)} %get-tuple-element.40), custom_call_target="InvertDiagBlocksLowerTriangular" | custom-call | tf_op jit(solution)/shard_map/jit(_solve_triangular)/triangular_solve | solution.py:75
  (231 shorter events, 341.9 us)
Async XLA Ops:
  7.2 72.8 %reduce-scatter.9.cloned.1.call-start = ((), (), s32[]{:S(2)}) async-start(), calls=%async_computation.8 | async-start | bytes 2621440 | tf_op jit(solution)/shard_map/reduce_scatter | solution.py:18
  28.0 13.0 copy-start.12
  46.0 55.2 %reduce-scatter.11.cloned.1.call-start = ((), (), s32[]{:S(2)}) async-start(), calls=%async_computation.9 | async-start | bytes 655360 | tf_op jit(solution)/shard_map/reduce_scatter | solution.py:18
  79.9 68.3 %all-gather.19.cloned.1.call-start = ((), (), s32[]{:S(2)}) async-start(), calls=%async_computation.10 | async-start | bytes 2621440 | tf_op jit(solution)/shard_map/all_gather | solution.py:24
  112.2 92.6 %all-gather.27.cloned.1.call-start = ((), (), s32[]{:S(2)}) async-start(), calls=%async_computation.21 | async-start | bytes 9437184 | tf_op jit(solution)/shard_map/all_gather | solution.py:33
  154.7 91.3 %reduce-scatter.13.cloned.1.call-start = ((), (), s32[]{:S(2)}) async-start(), calls=%async_computation.11 | async-start | bytes 2621440 | tf_op jit(solution)/shard_map/reduce_scatter | solution.py:18
  216.3 50.8 %copy-start.10 = (f32[64,512]{1,0:T(8,128)S(1)}, f32[64,512]{1,0:T(8,128)}, u32[]{:S(2)}) copy-start(f32[64,512]{1,0:T(8,128)} %reduce-scatter.11.cloned.1.call-done) | copy-start | bytes 393220
  216.4 50.8 %reduce-scatter.15.cloned.1.call-start = ((), (), s32[]{:S(2)}) async-start(), calls=%async_computation.12 | async-start | bytes 655360 | tf_op jit(solution)/shard_map/reduce_scatter | solution.py:18
  246.0 68.7 %all-gather.21.cloned.1.call-start = ((), (), s32[]{:S(2)}) async-start(), calls=%async_computation.13 | async-start | bytes 2621440 | tf_op jit(solution)/shard_map/all_gather | solution.py:24
  280.1 87.1 %all-gather.29.cloned.1.call-start = ((), (), s32[]{:S(2)}) async-start(), calls=%async_computation.22 | async-start | bytes 9437184 | tf_op jit(solution)/shard_map/all_gather | solution.py:29
  317.0 204.7 %all-reduce.5.cloned.1.call-start = ((), (), s32[]{:S(2)}) async-start(), calls=%async_computation.14 | async-start | bytes 2097152 | tf_op jit(solution)/shard_map/psum | solution.py:135
  370.2 320.7 %reduce-scatter.17.cloned.1.call-start = ((), (), s32[]{:S(2)}) async-start(), calls=%async_computation.15 | async-start | bytes 2621440 | tf_op jit(solution)/shard_map/reduce_scatter | solution.py:18
  568.5 86.0 %copy-start.3 = (f32[1,512,512]{1,2,0:T(8,128)S(1)}, f32[1,512,512]{1,2,0:T(8,128)}, u32[]{:S(2)}) copy-start(f32[1,512,512]{1,2,0:T(8,128)} %copy.61) | copy-start | bytes 3145732
  662.7 49.5 %reduce-scatter.19.cloned.1.call-start = ((), (), s32[]{:S(2)}) async-start(), calls=%async_computation.16 | async-start | bytes 655360 | tf_op jit(solution)/shard_map/reduce_scatter | solution.py:18
  690.9 68.3 %all-gather.23.cloned.1.call-start = ((), (), s32[]{:S(2)}) async-start(), calls=%async_computation.17 | async-start | bytes 2621440 | tf_op jit(solution)/shard_map/all_gather | solution.py:24
  723.2 93.2 %all-gather.31.cloned.1.call-start = ((), (), s32[]{:S(2)}) async-start(), calls=%async_computation.23 | async-start | bytes 9437184 | tf_op jit(solution)/shard_map/all_gather | solution.py:33
  766.2 92.0 %reduce-scatter.21.cloned.1.call-start = ((), (), s32[]{:S(2)}) async-start(), calls=%async_computation.18 | async-start | bytes 2621440 | tf_op jit(solution)/shard_map/reduce_scatter | solution.py:18
  828.6 50.8 %copy-start.9 = (f32[64,512]{1,0:T(8,128)S(1)}, f32[64,512]{1,0:T(8,128)}, u32[]{:S(2)}) copy-start(f32[64,512]{1,0:T(8,128)} %reduce-scatter.19.cloned.1.call-done) | copy-start | bytes 393220
  828.6 50.8 %reduce-scatter.23.cloned.1.call-start = ((), (), s32[]{:S(2)}) async-start(), calls=%async_computation.19 | async-start | bytes 655360 | tf_op jit(solution)/shard_map/reduce_scatter | solution.py:18
  858.2 68.7 %all-gather.25.cloned.1.call-start = ((), (), s32[]{:S(2)}) async-start(), calls=%async_computation.20 | async-start | bytes 2621440 | tf_op jit(solution)/shard_map/all_gather | solution.py:24
  892.4 87.2 %all-gather.33.cloned.1.call-start = ((), (), s32[]{:S(2)}) async-start(), calls=%async_computation.24 | async-start | bytes 9437184 | tf_op jit(solution)/shard_map/all_gather | solution.py:29
  929.4 101.5 %all-gather.35.cloned.1.call-start = ((), (), s32[]{:S(2)}) async-start(), calls=%async_computation.25 | async-start | bytes 9437184 | tf_op jit(solution)/shard_map/all_gather | solution.py:33
  936.0 255.0 %all-reduce.7.cloned.1.call-start = ((), (), s32[]{:S(2)}) async-start(), calls=%async_computation.26 | async-start | bytes 4194304 | tf_op jit(solution)/shard_map/psum | solution.py:135
  1276.9 49.3 %copy-start.6 = (f32[512,512]{0,1:T(8,128)S(1)}, f32[512,512]{0,1:T(8,128)}, u32[]{:S(2)}) copy-start(f32[512,512]{0,1:T(8,128)} %get-tuple-element.75) | copy-start | bytes 3145732
  (9 other events, 17.2 us)
Sparse Core Ops, SparseCore 0:
  46.1 33.7 reduce-scatter.8
  82.3 18.8 reduce-scatter.10
  112.4 35.8 all-gather.18
  154.8 50.0 all-gather.26
  216.5 29.4 reduce-scatter.12
  248.2 18.8 reduce-scatter.14
  280.3 34.4 all-gather.20
  317.1 50.0 all-gather.28
  372.0 149.6 all-reduce.4
  662.9 27.9 reduce-scatter.16
  693.2 18.9 reduce-scatter.18
  723.4 35.7 all-gather.22
  766.3 50.0 all-gather.30
  828.7 29.4 reduce-scatter.20
  860.5 18.8 reduce-scatter.22
  892.5 34.4 all-gather.24
  929.5 50.0 all-gather.32
  981.2 49.6 all-gather.34
  1038.5 152.4 all-reduce.6
where the time goes:
time: 1360 us; the launch traced here: 1350 us
  waiting for transfers between devices  887 us (65%)
  other arithmetic  256 us (19%)
  matrix products  75.1 us (6%)
  blocking collectives  74.8 us (6%)
  local copies, waits for them, and re-layouts  32.6 us (2%)
  between operations  22.6 us (2%)
    psum x2, waiting for transfers between devices, shards(): gram_total = lax.psum(gram_part, ROW_COL)  298 us
    reduce_scatter x8, waiting for transfers between devices, summed_rows(): total = lax.psum_scatter(total, axis, scatter_dimension=0, tiled=True)  206 us
    another operation x29, other arithmetic, shards(): factor = jnp.linalg.cholesky(gram_matrix)  158 us
    all_gather x3, waiting for transfers between devices, over_pieces(): pieces = lax.all_gather(array, axis)  148 us
    all_gather x4, waiting for transfers between devices, whole_of(): array = lax.all_gather(array, axis, axis=dim, tiled=True)  140 us
    all_gather x2, waiting for transfers between devices, broadcast(): lax.all_gather(array, axis)  93.5 us
    another operation x6, other arithmetic, tri_solve(): return jax.scipy.linalg.solve_triangular(factor, values, lower=True)  79.2 us
    all_gather x4, blocking collectives, whole_of(): array = lax.all_gather(array, axis, axis=dim, tiled=True)  46 us
  transfers between devices with their start and end apart: 19, of which 19 were waited for; matrix products, arithmetic and copies ran while one was open for 1% of the time, Pallas kernels for 0%

commit v1 on v0

v1 whole, which is shorter than its diff:
```python
import jax
import jax.numpy as jnp
from jax import lax
from jax.experimental import pallas as pl
from jax.experimental.pallas import tpu as pltpu
from jax.sharding import Mesh
from jax.sharding import PartitionSpec as P

ROW = ("row_0", "row_1")
COL = ("col_0", "col_1")
ROW_COL = ("row_0", "row_1", "col_0", "col_1")
COL_ROW = ("col_0", "col_1", "row_0", "row_1")
MESH = pl.DeviceIdType.MESH
F32 = jnp.float32
BF16 = jnp.bfloat16
VMEM_LIMIT = 62 * 1024 * 1024
LINKS = ("ya", "yb", "za", "zb"), ("yb", "ya", "zb", "za"), ("za", "zb", "ya", "yb"), ("zb", "za", "yb", "ya")


class Place:
    def __init__(self):
        self.x = lax.axis_index("row_0")
        self.core = lax.axis_index("row_1")
        self.z = lax.axis_index("col_0")
        self.y = lax.axis_index("col_1")
        self.at = {"x": self.x, "y": self.y, "z": self.z}

    def device(self, x=None, core=None, z=None, y=None):
        pick = lambda given, own: own if given is None else given
        return (pick(x, self.x), pick(core, self.core), pick(z, self.z), pick(y, self.y))

    def sibling(self):
        return self.device(core=1 - self.core)

    def partner(self, link):
        v = self.at[link[0]]
        w = v + 1 - 2 * (v % 2) if link[1] == "a" else 3 - v
        return self.device(**{link[0]: w})

    def bit(self, link):
        v = self.at[link[0]]
        return ((v + 1) // 2) % 2 if link[1] == "a" else v // 2


def remote(src, dst, send, recv, device):
    return pltpu.make_async_remote_copy(
        src_ref=src, dst_ref=dst, send_sem=send, recv_sem=recv, device_id=device, device_id_type=MESH
    )


def rows_at(start, size):
    return pl.ds(pl.multiple_of(start, size), size)


def halves(value):
    hi = value.astype(BF16)
    return hi, (value - hi.astype(F32)).astype(BF16)


def dot(left, right):
    return jnp.dot(left, right, preferred_element_type=F32)


def chain_kernel(
    interval, matrix, slab, y3_out, v3_out, z2_out,
    other, m_hi, m_lo, t_hi, t_lo, cols, rows, part, split_c, split_r,
    r1, h1, r2, h2, r3, h3, r4, share,
    tb, rb1, tb2, rb2, own3, got3,
    f_send, f_recv, b_send, b_recv, g_send, g_recv, m_send, m_recv, p_send, p_recv, s_send, s_recv,
):
    me = Place()
    block = me.z * 4 + me.y

    swap = remote(matrix, other, m_send, m_recv, me.sibling())
    swap.start()

    def slab_rows(x, core):
        return rows_at((x * 2 + core) * 64, 64)

    gathers = []
    for d in range(1, 8):
        to_x, to_core = (me.x + d // 2) % 4, (me.core + d) % 2
        for c in range(2):
            copy = remote(
                slab.at[2 * to_core + c], cols.at[0, c, slab_rows(me.x, me.core)],
                g_send.at[d, c], g_recv.at[d, c], me.device(x=to_x, core=to_core),
            )
            copy.start()
            gathers.append((d, c, copy))
    for c in range(2):
        cols[0, c, slab_rows(me.x, me.core), :] = slab[2 * me.core + c]

    center = 0.5 * (interval[0] + interval[1])
    half_width = 0.5 * (interval[1] - interval[0])

    def prepare(source, half):
        def tile(i, carry):
            base = half * 1024 + i * 256
            value = source[rows_at(i * 256, 256), :]
            row = me.x * 2048 + base + lax.broadcasted_iota(jnp.int32, (256, 512), 0)
            col = block * 512 + lax.broadcasted_iota(jnp.int32, (256, 512), 1)
            value = jnp.where(row == col, value - center, value) / half_width
            hi, lo = halves(value)
            where = rows_at(base, 256)
            m_hi[where, :] = hi
            m_lo[where, :] = lo
            hi, lo = halves(value.T)
            t_hi[:, where] = hi
            t_lo[:, where] = lo
            return carry

        lax.fori_loop(0, 4, tile, 0)

    prepare(matrix, me.core)
    swap.wait()
    prepare(other, 1 - me.core)
    for d, c, copy in gathers:
        copy.wait()

    def forward(c, f, source, target, before, last=False):
        hi, lo = halves(cols[source, c])
        split_c[c, :, :128] = hi
        split_c[c, :, 128:] = lo
        copies = {}

        def send(q, step, src, dst, link):
            copies[q, step] = remote(src, dst, f_send.at[f, c, q, step], f_recv.at[f, c, q, step], me.partner(link))
            copies[q, step].start()

        where1, where2 = [], []
        for q, (l1, l2, l3, l4) in enumerate(LINKS):
            strip = pl.ds(512 * q, 512)
            both = split_c[c]
            product = dot(m_hi[strip, :], both) + dot(m_lo[strip, :], both)
            part[c, strip, :] = product[:, :128] + product[:, 128:]
            k1, k2 = me.bit(l1), me.bit(l2)
            where1.append(512 * q + 256 * k1)
            where2.append(512 * q + 256 * k1 + 128 * k2)
            send(q, 0, part.at[c, rows_at(512 * q + 256 * (1 - k1), 256)], r1.at[f, c, q], l1)
        yield
        for q, (l1, l2, l3, l4) in enumerate(LINKS):
            k2 = me.bit(l2)
            copies[q, 0].wait_recv()
            h1[c, q] = part[c, rows_at(where1[q], 256), :] + r1[f, c, q]
            send(q, 1, h1.at[c, q, rows_at(128 * (1 - k2), 128)], r2.at[f, c, q], l2)
        yield
        for q, (l1, l2, l3, l4) in enumerate(LINKS):
            k2 = me.bit(l2)
            copies[q, 1].wait_recv()
            h2[c, q] = h1[c, q, rows_at(128 * k2, 128), :] + r2[f, c, q]
            send(q, 2, h2.at[c, q], r3.at[f, c, q], l3)
        yield
        for q, (l1, l2, l3, l4) in enumerate(LINKS):
            copies[q, 2].wait_recv()
            h3[c, q] = h2[c, q] + r3[f, c, q]
            send(q, 3, h3.at[c, q], r4.at[f, c, q], l4)
        yield
        if last:
            for q, (l1, l2, l3, l4) in enumerate(LINKS):
                copies[q, 3].wait_recv()
                share[c, q] = h3[c, q] + r4[f, c, q]
            for copy in copies.values():
                copy.wait_send()
            return
        for q, (l1, l2, l3, l4) in enumerate(LINKS):
            copies[q, 3].wait_recv()
            total = h3[c, q] + r4[f, c, q]
            here = rows_at(where2[q], 128)
            if before is not None:
                total = 2.0 * total - rows[before, c, here, :]
            rows[target, c, here, :] = total
            send(q, 4, rows.at[target, c, here], rows.at[target, c, here], l2)
        yield
        for q, (l1, l2, l3, l4) in enumerate(LINKS):
            copies[q, 4].wait_recv()
            here = rows_at(where1[q], 256)
            send(q, 5, rows.at[target, c, here], rows.at[target, c, here], l1)
        yield
        for q in range(4):
            copies[q, 5].wait_recv()
        for copy in copies.values():
            copy.wait_send()

    def backward(c, b, source, target, before):
        for i in range(4):
            strip = pl.ds(512 * i, 512)
            hi, lo = halves(rows[source, c, strip, :])
            split_r[c, strip, :128] = hi
            split_r[c, strip, 128:] = lo
        orders = ("xa", "xb"), ("xb", "xa")
        copies = {}

        def send(s, step, src, dst, link):
            copies[s, step] = remote(src, dst, b_send.at[b, c, s, step], b_recv.at[b, c, s, step], me.partner(link))
            copies[s, step].start()

        for s in range(2):
            strip = pl.ds(256 * s, 256)
            both = split_r[c]
            product = dot(t_hi[strip, :], both) + dot(t_lo[strip, :], both)
            tb[c, strip, :] = product[:, :128] + product[:, 128:]
            send(s, 0, tb.at[c, strip], rb1.at[b, c, strip], orders[s][0])
        yield
        for s in range(2):
            strip = pl.ds(256 * s, 256)
            copies[s, 0].wait_recv()
            tb2[c, strip, :] = tb[c, strip, :] + rb1[b, c, strip, :]
            send(s, 1, tb2.at[c, strip], rb2.at[b, c, strip], orders[s][1])
        yield
        for s in range(2):
            strip = pl.ds(256 * s, 256)
            copies[s, 1].wait_recv()
            total = tb2[c, strip, :] + rb2[b, c, strip, :]
            if before is not None:
                total = 2.0 * total - cols[before, c, strip, :]
            cols[target, c, strip, :] = total
        for copy in copies.values():
            copy.wait_send()

    def chain(c):
        yield from forward(c, 0, 0, 0, None)
        yield from backward(c, 0, 0, 1, 0)
        yield from forward(c, 1, 1, 1, 0)
        yield from backward(c, 1, 1, 2, None)
        yield from forward(c, 2, 2, 2, 1)
        yield from backward(c, 2, 2, 3, 2)
        yield from forward(c, 3, 3, None, None, last=True)
        pending = []
        for q, (l1, l2, l3, l4) in enumerate(LINKS):
            k1, k2, k3, k4 = me.bit(l1), me.bit(l2), me.bit(l3), me.bit(l4)
            to_x, to_y, to_z = 2 * k1 + k2, q, me.x
            index = 2 * k3 + k4
            same = (to_x == me.x) & (to_y == me.y) & (to_z == me.z)
            there = rows_at(32 * index, 32)
            copy = remote(
                share.at[c, q, there], own3.at[2, c, there],
                p_send.at[c, q], p_recv.at[c, index], me.device(x=to_x, y=to_y, z=to_z),
            )

            @pl.when(jnp.logical_not(same))
            def _():
                copy.start()

            @pl.when(same)
            def _():
                own3[2, c, there, :] = share[c, q, there, :]

            pending.append((same, copy))
        yield
        for same, copy in pending:

            @pl.when(jnp.logical_not(same))
            def _():
                copy.wait_send()

        own_index, own_same = None, None
        for q, (l1, l2, l3, l4) in enumerate(LINKS):
            k1, k2, k3, k4 = me.bit(l1), me.bit(l2), me.bit(l3), me.bit(l4)
            same = (2 * k1 + k2 == me.x) & (q == me.y) & (me.x == me.z)
            own_index = jnp.where(same, 2 * k3 + k4, own_index) if q else jnp.where(same, 2 * k3 + k4, -1)
        for index in range(4):

            @pl.when(own_index != index)
            def _():
                there = pl.ds(32 * index, 32)
                remote(
                    share.at[c, 0, there], own3.at[2, c, there], p_send.at[c, 0], p_recv.at[c, index], me.sibling()
                ).wait_recv()

    left, right = chain(0), chain(1)
    live = [left, right]
    for _ in range(LAG):
        next(left)
    while live:
        for one in list(live):
            if next(one, "end") == "end":
                live.remove(one)

    for c in range(2):
        own3[0, c] = rows[1, c, rows_at(block * 128, 128), :]
        own3[1, c] = cols[3, c, rows_at(me.x * 128, 128), :]
    final = remote(own3, got3, s_send, s_recv, me.sibling())
    final.start()
    final.wait()
    for k, out in enumerate((y3_out, v3_out, z2_out)):
        for c in range(2):

            @pl.when(me.core == 0)
            def _():
                out[:, pl.ds(128 * c, 128)] = own3[k, c]
                out[:, pl.ds(256 + 128 * c, 128)] = got3[k, c]

            @pl.when(me.core == 1)
            def _():
                out[:, pl.ds(128 * c, 128)] = got3[k, c]
                out[:, pl.ds(256 + 128 * c, 128)] = own3[k, c]


LAG = 3


def chain_call(matrix, slab, interval):
    vm = pl.BlockSpec(memory_space=pltpu.VMEM)
    dma = pltpu.SemaphoreType.DMA
    shape = jax.ShapeDtypeStruct((128, 512), F32)
    return pl.pallas_call(
        chain_kernel,
        out_shape=(shape, shape, shape),
        in_specs=[pl.BlockSpec(memory_space=pltpu.SMEM), vm, vm],
        out_specs=(vm, vm, vm),
        scratch_shapes=[
            pltpu.VMEM((1024, 512), F32),
            pltpu.VMEM((2048, 512), BF16),
            pltpu.VMEM((2048, 512), BF16),
            pltpu.VMEM((512, 2048), BF16),
            pltpu.VMEM((512, 2048), BF16),
            pltpu.VMEM((4, 2, 512, 128), F32),
            pltpu.VMEM((3, 2, 2048, 128), F32),
            pltpu.VMEM((2, 2048, 128), F32),
            pltpu.VMEM((2, 512, 256), BF16),
            pltpu.VMEM((2, 2048, 256), BF16),
            pltpu.VMEM((4, 2, 4, 256, 128), F32),
            pltpu.VMEM((2, 4, 256, 128), F32),
            pltpu.VMEM((4, 2, 4, 128, 128), F32),
            pltpu.VMEM((2, 4, 128, 128), F32),
            pltpu.VMEM((4, 2, 4, 128, 128), F32),
            pltpu.VMEM((2, 4, 128, 128), F32),
            pltpu.VMEM((4, 2, 4, 128, 128), F32),
            pltpu.VMEM((2, 4, 128, 128), F32),
            pltpu.VMEM((2, 512, 128), F32),
            pltpu.VMEM((3, 2, 512, 128), F32),
            pltpu.VMEM((2, 512, 128), F32),
            pltpu.VMEM((3, 2, 512, 128), F32),
            pltpu.VMEM((3, 2, 128, 128), F32),
            pltpu.VMEM((3, 2, 128, 128), F32),
            dma((4, 2, 4, 6)),
            dma((4, 2, 4, 6)),
            dma((3, 2, 2, 2)),
            dma((3, 2, 2, 2)),
            dma((8, 2)),
            dma((8, 2)),
            dma,
            dma,
            dma((2, 4)),
            dma((2, 4)),
            dma,
            dma,
        ],
        compiler_params=pltpu.CompilerParams(has_side_effects=True, vmem_limit_bytes=VMEM_LIMIT),
    )(interval, matrix, slab)


def product(left, right):
    return jnp.dot(left, right, precision=lax.Precision.HIGHEST, preferred_element_type=jnp.float32)


def tri_solve(factor, values):
    return jax.scipy.linalg.solve_triangular(factor, values, lower=True)


def shards(matrix, start_vectors, interval):
    pieces = start_vectors.reshape(64, 4, 128).transpose(1, 0, 2)
    total_rows = start_vectors.shape[0] * lax.axis_size(ROW) * lax.axis_size(COL)
    y3, v3, z2 = chain_call(matrix, pieces, interval)
    core = lax.axis_index("row_1")
    mine = lambda a: lax.dynamic_slice_in_dim(a, core * 64, 64, 0)
    y3, v3, z2 = mine(y3), mine(v3), mine(z2)
    first = jnp.linalg.cholesky(lax.psum(product(y3.T, y3), ROW_COL) / total_rows)
    filtered = tri_solve(first, v3.T).T
    mapped = tri_solve(first, z2.T).T
    gram, cross = lax.psum((product(filtered.T, filtered), product(filtered.T, mapped)), ROW_COL)
    factor = jnp.linalg.cholesky(gram / total_rows)
    basis = tri_solve(factor, filtered.T).T
    projected = tri_solve(factor, tri_solve(factor, cross / total_rows).T).T
    residual = tri_solve(factor, mapped.T).T - product(basis, projected)
    return basis, projected, residual


def solution(mesh):
    torus = Mesh(mesh.devices.reshape(4, 2, 4, 4), ("row_0", "row_1", "col_0", "col_1"))
    placed = (P(ROW, COL), P(COL_ROW, None), P())
    return jax.shard_map(
        shards,
        mesh=torus,
        in_specs=placed,
        out_specs=(P(COL_ROW, None), P(), P(COL_ROW, None)),
        check_vma=False,
    )
```

time: 1360 us -> 827 us (0.61)
  waiting for transfers between devices: 887 us -> 299 us
  Pallas kernels: 0 us -> 207 us
  blocking collectives: 74.8 us -> 0 us
  matrix products: 75.1 us -> 28.6 us
  other arithmetic: 256 us -> 242 us
    all_gather x9 -> x0, waiting for transfers between devices: 382 us -> none  [the longest x3 148 us: over_pieces(): pieces = lax.all_gather(array, axis)]
    pallas_call x0 -> x1, Pallas kernels: none -> 207 us  [chain_call(): pl.pallas_call(chain_kernel, out_shape=(shape, shape, shape), in_specs=[p...]
    reduce_scatter x8 -> x0, waiting for transfers between devices: 206 us -> none  [summed_rows(): total = lax.psum_scatter(total, axis, scatter_dimension=0, tiled=True)]
    all_gather x8 -> x0, blocking collectives: 74.8 us -> none  [the longest x4 46 us: whole_of(): array = lax.all_gather(array, axis, axis=dim, tiled=True)]
    dot_general x8 -> x4, matrix products: 34 us -> 8.8 us  [product(): jnp.dot(left, right, precision=lax.Precision.HIGHEST, preferred_element_t...]
    dot_general x3 -> x0, matrix products: 20 us -> none  [backward(): lax.dot_general(shifted, row_full, (((0,), (0,)), ((), ())), precision=la...]
    another operation x6 -> x5, other arithmetic: 79.2 us -> 78.9 us  [tri_solve(): return jax.scipy.linalg.solve_triangular(factor, values, lower=True)]
  transfers between devices with their start and end apart: 19 -> 2, of which waited for: 19 -> 2; matrix products, arithmetic and copies ran while one was open for 1% -> 0% of each run, Pallas kernels for 0% -> 0%
where the time goes in v1:
time: 827 us; the launch traced here: 817 us
  waiting for transfers between devices  299 us (36%)
  other arithmetic  242 us (29%)
  Pallas kernels  207 us (25%)
  matrix products  28.6 us (3%)
  local copies, waits for them, and re-layouts  20.8 us (3%)
  between operations  20 us (2%)
    pallas_call x1, Pallas kernels, chain_call(): pl.pallas_call(chain_kernel, out_shape=(shape, shape, shape), in_specs=[p...  207 us
    psum x1, waiting for transfers between devices, shards(): lax.psum((product(filtered.T, filtered), product(filtered.T, mapped)), RO...  151 us
    psum x1, waiting for transfers between devices, shards(): lax.psum(product(y3.T, y3), ROW_COL) / total_rows  148 us
    another operation x15, other arithmetic, shards(): factor = jnp.linalg.cholesky(gram / total_rows)  79.6 us
    another operation x14, other arithmetic, shards(): jnp.linalg.cholesky(lax.psum(product(y3.T, y3), ROW_COL) / total_rows)  79 us
    another operation x5, other arithmetic, tri_solve(): return jax.scipy.linalg.solve_triangular(factor, values, lower=True)  78.9 us
  transfers between devices with their start and end apart: 2, of which 2 were waited for; matrix products, arithmetic and copies ran while one was open for 0% of the time, Pallas kernels for 0%

profile of v1, /device:TPU:1, one launch (start us, length us, event | category | flops | bytes accessed | tf_op | source)
XLA Modules:
  0.0 817.4 jit_solution(14392930141539852995)
XLA Ops:
  8.7 207.1 %shard_map.58 = (f32[128,512]{1,0:T(8,128)}, f32[128,512]{1,0:T(8,128)}, f32[128,512]{1,0:T(8,128)}) custom-call(f32[2]{0:T(128)} %interval.1, f32[1024,512]{1,0:T(8,128)} %matrix.1, f32[4,64,128]{2,1,0:T(8,128)} %bitcast_bitcast_fusion.slab), custom_call_target="tpu_custom_call" | custom-call | tf_op jit(solution)/shard_map/pallas_call | solution.py:306
  215.9 3.0 fusion.49
  219.9 147.6 %all-reduce.5.cloned.1.call-done = f32[512,512]{0,1:T(8,128)} async-done(((f32[512,512]{0,1:T(8,128)}), f32[512,512]{0,1:T(8,128)}) %all-reduce.5.cloned.1.call-update) | async-done | bytes 1048592 | tf_op jit(solution)/shard_map/psum | solution.py:368
  369.5 11.7 %cholesky.286 = f32[128,128]{1,0:T(8,128)S(1)} custom-call(f32[128,128]{1,0:T(8,128)S(1)} %cholesky.426), custom_call_target="Cholesky" | custom-call | tf_op jit(solution)/shard_map/jit(cholesky)/cholesky | solution.py:368
  381.3 9.8 %custom-call.33 = f32[1,128,128]{1,2,0:T(8,128)S(1)} custom-call(f32[1,128,128]{2,1,0:T(8,128)S(1)} %get-tuple-element.105), custom_call_target="InvertDiagBlocksLowerTriangular" | custom-call | tf_op jit(solution)/shard_map/jit(cholesky)/cholesky | solution.py:368
  391.9 11.7 %cholesky.305 = f32[128,128]{1,0:T(8,128)S(1)} custom-call(f32[128,128]{1,0:T(8,128)S(1)} %cholesky.430), custom_call_target="Cholesky" | custom-call | tf_op jit(solution)/shard_map/jit(cholesky)/cholesky | solution.py:368
  403.6 10.3 %custom-call.34 = f32[1,128,128]{1,2,0:T(8,128)S(1)} custom-call(f32[1,128,128]{2,1,0:T(8,128)S(1)} %get-tuple-element.102), custom_call_target="InvertDiagBlocksLowerTriangular" | custom-call | tf_op jit(solution)/shard_map/jit(cholesky)/cholesky | solution.py:368
  414.6 11.7 %cholesky.326 = f32[128,128]{1,0:T(8,128)S(1)} custom-call(f32[128,128]{1,0:T(8,128)S(1)} %cholesky.435), custom_call_target="Cholesky" | custom-call | tf_op jit(solution)/shard_map/jit(cholesky)/cholesky | solution.py:368
  427.0 9.8 %custom-call.35 = f32[1,128,128]{1,2,0:T(8,128)S(1)} custom-call(f32[1,128,128]{2,1,0:T(8,128)S(1)} %get-tuple-element.99), custom_call_target="InvertDiagBlocksLowerTriangular" | custom-call | tf_op jit(solution)/shard_map/jit(cholesky)/cholesky | solution.py:368
  437.5 11.7 %cholesky.343 = f32[128,128]{1,0:T(8,128)S(1)} custom-call(f32[128,128]{1,0:T(8,128)S(1)} %convolution_subtract_fusion.12), custom_call_target="Cholesky" | custom-call | tf_op jit(solution)/shard_map/jit(cholesky)/cholesky | solution.py:368
  453.4 8.5 %while.12 = (s32[]{:T(128)}, f32[512,512]{1,0:T(8,128)S(1)}, s32[4,2]{0,1:T(2,128)S(1)}, f32[4,128,128]{2,1,0:T(8,128)S(1)}, s32[]{:T(128)}) while((s32[]{:T(128)}, f32[512,512]{1,0:T(8,128)S(1)}, s32[4,2]{0,1:T(2,128)S(1)}, f32[4,128,128]{2,1,0:T(8,128)S(1)}, s32[]{:T(128)}) %tuple.72), condition=%wide.while_cond, body=%wide.while_body.sunk | while | flops 2 | bytes 131181 | solution.py:358
  461.9 39.3 %custom-call.36 = f32[4,128,128]{1,2,0:T(8,128)S(1)} custom-call(f32[4,128,128]{2,1,0:T(8,128)S(1)} %get-tuple-element.52), custom_call_target="InvertDiagBlocksLowerTriangular" | custom-call | tf_op jit(solution)/shard_map/jit(_solve_triangular)/triangular_solve | solution.py:358
  504.6 2.0 fusion.78
  506.6 2.0 fusion.41
  508.6 151.0 %all-reduce.7.cloned.1.call-done = (f32[512,512]{0,1:T(8,128)}, f32[512,512]{0,1:T(8,128)}) async-done(((f32[512,512]{0,1:T(8,128)}, f32[512,512]{0,1:T(8,128)}), (f32[512,512]{0,1:T(8,128)}, f32[512,512]{0,1:T(8,128)})) %all-reduce.7.cloned.1.call-update) | async-done | bytes 2097168 | tf_op jit(solution)/shard_map/psum | solution.py:371
  661.6 11.7 %cholesky.358 = f32[128,128]{1,0:T(8,128)S(1)} custom-call(f32[128,128]{1,0:T(8,128)S(1)} %cholesky.439), custom_call_target="Cholesky" | custom-call | tf_op jit(solution)/shard_map/jit(cholesky)/cholesky | solution.py:372
  673.5 9.8 %custom-call.37 = f32[1,128,128]{1,2,0:T(8,128)S(1)} custom-call(f32[1,128,128]{2,1,0:T(8,128)S(1)} %get-tuple-element.95), custom_call_target="InvertDiagBlocksLowerTriangular" | custom-call | tf_op jit(solution)/shard_map/jit(cholesky)/cholesky | solution.py:372
  684.0 12.1 %cholesky.377 = f32[128,128]{1,0:T(8,128)S(1)} custom-call(f32[128,128]{1,0:T(8,128)S(1)} %cholesky.443), custom_call_target="Cholesky" | custom-call | tf_op jit(solution)/shard_map/jit(cholesky)/cholesky | solution.py:372
  697.4 9.8 %custom-call.38 = f32[1,128,128]{1,2,0:T(8,128)S(1)} custom-call(f32[1,128,128]{2,1,0:T(8,128)S(1)} %get-tuple-element.92), custom_call_target="InvertDiagBlocksLowerTriangular" | custom-call | tf_op jit(solution)/shard_map/jit(cholesky)/cholesky | solution.py:372
  707.9 11.7 %cholesky.398 = f32[128,128]{1,0:T(8,128)S(1)} custom-call(f32[128,128]{1,0:T(8,128)S(1)} %cholesky.448), custom_call_target="Cholesky" | custom-call | tf_op jit(solution)/shard_map/jit(cholesky)/cholesky | solution.py:372
  720.3 9.8 %custom-call.39 = f32[1,128,128]{1,2,0:T(8,128)S(1)} custom-call(f32[1,128,128]{2,1,0:T(8,128)S(1)} %get-tuple-element.89), custom_call_target="InvertDiagBlocksLowerTriangular" | custom-call | tf_op jit(solution)/shard_map/jit(cholesky)/cholesky | solution.py:372
  730.8 11.9 %cholesky.415 = f32[128,128]{1,0:T(8,128)S(1)} custom-call(f32[128,128]{1,0:T(8,128)S(1)} %convolution_subtract_fusion.11), custom_call_target="Cholesky" | custom-call | tf_op jit(solution)/shard_map/jit(cholesky)/cholesky | solution.py:372
  746.0 8.0 while.13
  754.0 39.3 %custom-call.40 = f32[4,128,128]{1,2,0:T(8,128)S(1)} custom-call(f32[4,128,128]{2,1,0:T(8,128)S(1)} %get-tuple-element.53), custom_call_target="InvertDiagBlocksLowerTriangular" | custom-call | tf_op jit(solution)/shard_map/jit(_solve_triangular)/triangular_solve | solution.py:358
  (139 shorter events, 52.3 us)
Async XLA Ops:
  7.2 0.9 copy-start
  7.2 360.3 %all-reduce.5.cloned.1.call-start = ((), (), s32[]{:S(2)}) async-start(), calls=%async_computation | async-start | bytes 2097152 | tf_op jit(solution)/shard_map/psum | solution.py:368
  215.8 3.3 copy-start.5
  215.8 3.3 copy-start.6
  218.9 440.7 %all-reduce.7.cloned.1.call-start = ((), (), s32[]{:S(2)}) async-start(), calls=%async_computation.1 | async-start | bytes 4194304 | tf_op jit(solution)/shard_map/psum | solution.py:371
  367.5 1.8 copy-start.1
  453.2 49.7 %copy-start.4 = (f32[512,64]{0,1:T(8,128)S(1)}, f32[512,64]{0,1:T(8,128)}, u32[]{:S(2)}) copy-start(f32[512,64]{0,1:T(8,128)} %get-tuple-element.111) | copy-start | bytes 393220
  659.6 1.8 copy-start.2
  745.9 49.4 %copy-start.3 = (f32[512,512]{0,1:T(8,128)S(1)}, f32[512,512]{0,1:T(8,128)}, u32[]{:S(2)}) copy-start(f32[512,512]{0,1:T(8,128)} %get-tuple-element.81) | copy-start | bytes 3145732
Sparse Core Ops, SparseCore 0:
  219.0 148.4 all-reduce.4
  508.7 150.8 all-reduce.6
